TPU v7x, 128 devices: a whole 4x4x4 slice. The times are simulated.
128 devices in a mesh: worker: 4 (over y_hi, core), outer: 4 (over x), mp: 8 (over y_lo, z).
Axes of the slice: x: 4, y: 4 (y_hi: 2, y_lo: 2; y = y_hi * 2 + y_lo), z: 4, core: 2. Of those that a mesh axis runs over, the one named last changes fastest.
Arguments:
- grads: float32 [4, 4, 3584, 4096], P('worker', 'outer', None, 'mp'), as said below
- center: float32 [3584, 4096], P(('worker', 'outer'), 'mp'), may hold values from -6 to 6
- radius: float32 [1], replicated, may hold values from 1.5 to 3.5
Outputs:
- center_out: float32 [3584, 4096], P(('worker', 'outer'), 'mp')
Inputs may be any that keep to these rules, and one draw needn't show every extreme that they name: `grads`: finite values.
All inputs are finite; a program needn't handle non-finite values.
Results may differ from a plain program's by a relative error of at most 0.0001.
Values sent between devices are 32-bit elements; how exact they have to be, the bound alone decides.
A program may use at most 128 MiB of HBM per device.

v0:
```python
import functools
import math

import jax
import jax.numpy as jnp
from jax import lax
from jax.sharding import Mesh
from jax.sharding import PartitionSpec as P

D = 3584
ITERS = 2
KVW = 4096
WORKER = ("worker_0", "worker_1")
WORKER_OUTER = ("worker_0", "worker_1", "outer")
WORKER_OUTER_MP = ("worker_0", "worker_1", "outer", "mp_0", "mp_1")
MP = ("mp_0", "mp_1")


epsilon = 1e-06


def cut_along(value, dim, peers):
    before, after = (value.shape[:dim], value.shape[dim + 1 :])
    return jnp.moveaxis(value.reshape(*before, peers, -1, *after), dim, 0)


def piece_ends(length, count):
    unit = 8 if length >= 8 * count else 1
    return [length // unit * k // count * unit for k in range(1, count)]


def in_order(pieces, dim):
    pieces = jnp.moveaxis(pieces, 0, dim)
    shape = pieces.shape
    return pieces.reshape(*shape[:dim], shape[dim] * shape[dim + 1], *shape[dim + 2 :])


def cut_exchange(value, axis, pieces, split_dim, concat_dim):
    blocks = cut_along(value, split_dim, lax.axis_size(axis))
    cut = max(range(1, max(2, blocks.ndim - 1)), key=lambda d: blocks.shape[d])
    done = []
    for section in jnp.split(blocks, piece_ends(blocks.shape[cut], pieces), axis=cut):
        if section.size:
            done.append(lax.all_to_all(section, axis, split_axis=0, concat_axis=0, tiled=True))
    return in_order(jnp.concatenate(done, axis=cut), concat_dim)


def over_axes(value, axes):
    return functools.reduce(lax.psum, axes, value)


def on_device(grads, center, radius):
    worker_count = lax.axis_size(WORKER) * lax.axis_size("outer")
    radius_total = radius[0] * math.sqrt(D * KVW)
    own_rows = center
    mine = grads.reshape(1, grads.shape[2], grads.shape[3])
    gathered = cut_exchange(mine, WORKER_OUTER, 2, 1, 0)
    for iteration in range(ITERS):
        difference = gathered - own_rows[None]
        partial_value = jnp.sum(difference * difference, axis=(1, 2))
        norm_sq = over_axes(partial_value, WORKER_OUTER_MP)
        factor = jnp.minimum(1.0, radius_total * lax.rsqrt(norm_sq + epsilon))
        summed = jnp.sum(factor[:, None, None] * difference, axis=0)
        own_rows = own_rows + summed / worker_count
    return own_rows


def solution(mesh):
    split = Mesh(
        mesh.devices.reshape(2, 2, mesh.shape["outer"], 2, 4),
        ("worker_0", "worker_1", "outer", "mp_0", "mp_1"),
    )
    placed = (P(WORKER, "outer", None, MP), P(WORKER_OUTER, MP), P())
    return jax.shard_map(
        on_device, mesh=split, in_specs=placed, out_specs=P(WORKER_OUTER, MP), check_vma=False
    )
```

profile of v0, /device:TPU:0, one launch (start us, length us, event | category | flops | bytes accessed | tf_op | source)
XLA Modules:
  0.0 194.5 jit_solution(3620327716308379419)
XLA Ops:
  0.0 6.4 %fusion = (f32[16,1,112,512]{3,2,1,0:T(8,128)S(1)}, f32[16,1,112,512]{3,2,1,0:T(8,128)}) fusion(f32[16,1,224,512]{3,2,1,0:T(8,128)} %bitcast.12), kind=kLoop, calls=%fused_computation.9 | loop fusion | bytes 14680064 | tf_op jit(solution)/shard_map/split | solution.py:42
  6.4 0.0 copy-start.1
  6.4 53.2 %all_to_all.10 = f32[16,1,112,512]{3,2,1,0:T(8,128)} all-to-all(f32[16,1,112,512]{3,2,1,0:T(8,128)S(1)} %get-tuple-element.5), channel_id=1, replica_groups=mesh['worker_0'=2,'worker_1'=2,'outer'=4,'mp_0'=2,'mp_1'=4] {'worker_0',..., dimensions={0} | all-to-all | bytes 7340032 | tf_op jit(solution)/shard_map/all_to_all | solution.py:44
  59.6 4.5 %all-to-all-start.1 = ((f32[16,1,112,512]{3,2,1,0:T(8,128)}), f32[16,1,112,512]{3,2,1,0:T(8,128)}, u32[]{:S(2)}, u32[]{:S(2)}) async-start(f32[16,1,112,512]{3,2,1,0:T(8,128)} %get-tuple-element.6), calls=%async_computation.1 | async-start | bytes 7340032 | tf_op jit(solution)/shard_map/all_to_all | solution.py:44
  64.8 50.0 %all-to-all-done.1 = f32[16,1,112,512]{3,2,1,0:T(8,128)} async-done(((f32[16,1,112,512]{3,2,1,0:T(8,128)}), f32[16,1,112,512]{3,2,1,0:T(8,128)}, u32[]{:S(2)}, u32[]{:S(2)}) %all-to-all-start.1) | async-done | bytes 3670048 | tf_op jit(solution)/shard_map/all_to_all | solution.py:44
  114.8 0.0 copy-done.1
  114.8 3.8 %multiply_reduce_fusion.3 = f32[16]{0:T(128)S(1)} fusion(f32[224,512]{1,0:T(8,128)S(1)} %copy-done.1, f32[16,1,112,512]{3,2,1,0:T(8,128)} %all-to-all-done.1, f32[16,1,112,512]{3,2,1,0:T(8,128)} %all_to_all.10), kind=kLoop, calls=%fused_computation.4 | loop fusion | flops 7340016 | bytes 7798848 | tf_op jit(solution)/shard_map/reduce_sum | solution.py:60
  118.5 6.4 %psum.70 = f32[16]{0:T(128)S(1)} all-reduce(f32[16]{0:T(128)S(1)} %multiply_reduce_fusion.3), channel_id=1, replica_groups=mesh['worker_0'=2,'worker_1'=2,'outer'=4,'mp_0'=2,'mp_1'=4] {'worker_0'}, use_global_device_ids=true, to_apply=%region_1.0 | all-reduce | flops 16 | bytes 128 | tf_op jit(solution)/shard_map/psum | solution.py:49
  125.0 2.4 %psum.71 = f32[16]{0:T(128)S(1)} all-reduce(f32[16]{0:T(128)S(1)} %psum.70), channel_id=1, replica_groups=mesh['worker_0'=2,'worker_1'=2,'outer'=4,'mp_0'=2,'mp_1'=4] {'worker_1'}, use_global_device_ids=true, to_apply=%region_2.0 | all-reduce | flops 16 | bytes 128 | tf_op jit(solution)/shard_map/psum | solution.py:49
  127.4 7.7 %psum.72 = f32[16]{0:T(128)S(1)} all-reduce(f32[16]{0:T(128)S(1)} %psum.71), channel_id=1, replica_groups=mesh['worker_0'=2,'worker_1'=2,'outer'=4,'mp_0'=2,'mp_1'=4] {'outer'}, use_global_device_ids=true, to_apply=%region_3.0 | all-reduce | flops 16 | bytes 128 | tf_op jit(solution)/shard_map/psum | solution.py:49
  135.1 4.9 %psum.73 = f32[16]{0:T(128)S(1)} all-reduce(f32[16]{0:T(128)S(1)} %psum.72), channel_id=1, replica_groups=mesh['worker_0'=2,'worker_1'=2,'outer'=4,'mp_0'=2,'mp_1'=4] {'mp_0'}, use_global_device_ids=true, to_apply=%region_4.0 | all-reduce | flops 16 | bytes 128 | tf_op jit(solution)/shard_map/psum | solution.py:49
  140.0 11.7 %psum.74 = f32[16]{0:T(128)S(1)} all-reduce(f32[16]{0:T(128)S(1)} %psum.73), channel_id=1, replica_groups=mesh['worker_0'=2,'worker_1'=2,'outer'=4,'mp_0'=2,'mp_1'=4] {'mp_1'}, use_global_device_ids=true, to_apply=%region_5.0 | all-reduce | flops 16 | bytes 128 | tf_op jit(solution)/shard_map/psum | solution.py:49
  151.8 0.0 copy-start
  151.8 4.1 %multiply_reduce_fusion.2 = f32[224,512]{1,0:T(8,128)S(1)} fusion(f32[16]{0:T(128)S(1)} %multiply_minimum_fusion.1, f32[224,512]{1,0:T(8,128)S(1)} %copy-done.1, f32[16,1,112,512]{3,2,1,0:T(8,128)} %all-to-all-done.1, f32[16,1,112,512]{3,2,1,0:T(8,128)} %all_to_all.10), kind=kLoop, calls=%fused_computation.3 | loop fusion | flops 7225344 | bytes 8257600 | tf_op jit(solution)/shard_map/reduce_sum | solution.py:63
  155.9 0.1 multiply_add_fusion.1
  155.9 0.0 copy-done
  156.0 2.6 %multiply_reduce_fusion.1 = f32[16]{0:T(128)S(1)} fusion(f32[224,512]{1,0:T(8,128)S(1)} %multiply_add_fusion.1, f32[16,1,112,512]{3,2,1,0:T(8,128)} %all-to-all-done.1, f32[16,1,112,512]{3,2,1,0:T(8,128)S(1)} %copy-done), kind=kLoop, calls=%fused_computation.2 | loop fusion | flops 7340016 | bytes 7798848 | tf_op jit(solution)/shard_map/reduce_sum | solution.py:60
  158.6 6.4 %psum.75 = f32[16]{0:T(128)S(1)} all-reduce(f32[16]{0:T(128)S(1)} %multiply_reduce_fusion.1), channel_id=1, replica_groups=mesh['worker_0'=2,'worker_1'=2,'outer'=4,'mp_0'=2,'mp_1'=4] {'worker_0'}, use_global_device_ids=true, to_apply=%region_8.0 | all-reduce | flops 16 | bytes 128 | tf_op jit(solution)/shard_map/psum | solution.py:49
  165.0 2.4 %psum.76 = f32[16]{0:T(128)S(1)} all-reduce(f32[16]{0:T(128)S(1)} %psum.75), channel_id=1, replica_groups=mesh['worker_0'=2,'worker_1'=2,'outer'=4,'mp_0'=2,'mp_1'=4] {'worker_1'}, use_global_device_ids=true, to_apply=%region_9.0 | all-reduce | flops 16 | bytes 128 | tf_op jit(solution)/shard_map/psum | solution.py:49
  167.5 9.7 %psum.77 = f32[16]{0:T(128)S(1)} all-reduce(f32[16]{0:T(128)S(1)} %psum.76), channel_id=1, replica_groups=mesh['worker_0'=2,'worker_1'=2,'outer'=4,'mp_0'=2,'mp_1'=4] {'outer'}, use_global_device_ids=true, to_apply=%region_10.0 | all-reduce | flops 16 | bytes 128 | tf_op jit(solution)/shard_map/psum | solution.py:49
  177.2 4.9 %psum.78 = f32[16]{0:T(128)S(1)} all-reduce(f32[16]{0:T(128)S(1)} %psum.77), channel_id=1, replica_groups=mesh['worker_0'=2,'worker_1'=2,'outer'=4,'mp_0'=2,'mp_1'=4] {'mp_0'}, use_global_device_ids=true, to_apply=%region_11.0 | all-reduce | flops 16 | bytes 128 | tf_op jit(solution)/shard_map/psum | solution.py:49
  182.1 7.7 %psum.79 = f32[16]{0:T(128)S(1)} all-reduce(f32[16]{0:T(128)S(1)} %psum.78), channel_id=1, replica_groups=mesh['worker_0'=2,'worker_1'=2,'outer'=4,'mp_0'=2,'mp_1'=4] {'mp_1'}, use_global_device_ids=true, to_apply=%region_12.0 | all-reduce | flops 16 | bytes 128 | tf_op jit(solution)/shard_map/psum | solution.py:49
  189.8 3.8 %multiply_reduce_fusion = f32[224,512]{1,0:T(8,128)S(1)} fusion(f32[16]{0:T(128)S(1)} %multiply_minimum_fusion, f32[224,512]{1,0:T(8,128)S(1)} %multiply_add_fusion.1, f32[16,1,112,512]{3,2,1,0:T(8,128)} %all-to-all-done.1, f32[16,1,112,512]{3,2,1,0:T(8,128)} %all_to_all.10), kind=kLoop, calls=%fused_computation.1 | loop fusion | flops 7225344 | bytes 8257600 | tf_op jit(solution)/shard_map/reduce_sum | solution.py:63
  193.7 0.8 multiply_add_fusion
  (2 shorter events, 0.0 us)
Async XLA Ops:
  6.4 108.4 %copy-start.1 = (f32[224,512]{1,0:T(8,128)S(1)}, f32[224,512]{1,0:T(8,128)}, u32[]{:S(2)}) copy-start(f32[224,512]{1,0:T(8,128)} %param.4) | copy-start | bytes 1376260
  59.6 55.2 %all-to-all-start.1 = ((f32[16,1,112,512]{3,2,1,0:T(8,128)}), f32[16,1,112,512]{3,2,1,0:T(8,128)}, u32[]{:S(2)}, u32[]{:S(2)}) async-start(f32[16,1,112,512]{3,2,1,0:T(8,128)} %get-tuple-element.6), calls=%async_computation.1 | async-start | bytes 7340032 | tf_op jit(solution)/shard_map/all_to_all | solution.py:44
  151.8 4.2 %copy-start = (f32[16,1,112,512]{3,2,1,0:T(8,128)S(1)}, f32[16,1,112,512]{3,2,1,0:T(8,128)}, u32[]{:S(2)}) copy-start(f32[16,1,112,512]{3,2,1,0:T(8,128)} %all_to_all.10) | copy-start | bytes 11010052
where the time goes:
time: 195 us; the launch traced here: 194 us
  blocking collectives  118 us (61%)
  waiting for transfers between devices  50 us (26%)
  other arithmetic  15.3 us (8%)
  local copies, waits for them, and re-layouts  6.39 us (3%)
  starting transfers between devices  4.5 us (2%)
    psum x10, blocking collectives, over_axes(): return functools.reduce(lax.psum, axes, value)  64.4 us
    all_to_all x1, blocking collectives, cut_exchange(): lax.all_to_all(section, axis, split_axis=0, concat_axis=0, tiled=True)  53.2 us
    all_to_all x1, waiting for transfers between devices, cut_exchange(): lax.all_to_all(section, axis, split_axis=0, concat_axis=0, tiled=True)  50 us
    reduce_sum x2, other arithmetic, on_device(): summed = jnp.sum(factor[:, None, None] * difference, axis=0)  7.9 us
    reduce_sum x2, other arithmetic, on_device(): partial_value = jnp.sum(difference * difference, axis=(1, 2))  6.42 us
    split x1, local copies, waits for them, and re-layouts, cut_exchange(): jnp.split(blocks, piece_ends(blocks.shape[cut], pieces), axis=cut)  6.36 us
    all_to_all x1, starting transfers between devices, cut_exchange(): lax.all_to_all(section, axis, split_axis=0, concat_axis=0, tiled=True)  4.5 us
  transfers between devices with their start and end apart: 1, of which 1 were waited for; matrix products, arithmetic and copies ran while one was open for 0% of the time, Pallas kernels for 0%

commit v1 on v0

v1 whole, which is shorter than its diff:
```python
import functools
import math

import jax
import jax.numpy as jnp
from jax import lax
from jax.experimental import pallas as pl
from jax.experimental.pallas import tpu as pltpu
from jax.sharding import PartitionSpec as P

MESH = pl.DeviceIdType.MESH
D = 3584
KVW = 4096
WORKERS = 16
MP = 8
EPS = 1e-06
CHUNKS = 7
LANES = 128
BLOCK = 4


def send_order():
    order = []
    for core in (0, 1):
        for flip in (0, 1):
            for step in (1, 3, 2):
                order.append((flip, step, core))
            if core == 1:
                order.append((flip, 0, core))
    return order


def kernel(rows, chunk, grads, center, radius, out, held, start, acc, bias, mine, group, half, lines, sent, landed, near, scalar_sent, scalar_landed):
    w, o, m = lax.axis_index("worker"), lax.axis_index("outer"), lax.axis_index("mp")
    high, core = w // 2, w % 2
    me = w * 4 + o

    own = pltpu.make_async_copy(grads.at[pl.ds(pl.multiple_of(me * rows, 8), rows)], held.at[me], near.at[0])
    base = pltpu.make_async_copy(center, start, near.at[1])
    own.start()
    base.start()

    barrier = pltpu.get_barrier_semaphore()
    for k in range(1, WORKERS):
        pl.semaphore_signal(barrier, inc=1, device_id=((w + k // 4) % 4, (o + k % 4) % 4, m), device_id_type=MESH)
    for k in range(1, MP):
        pl.semaphore_signal(barrier, inc=1, device_id=(w, o, (m + k) % MP), device_id_type=MESH)
    pl.semaphore_wait(barrier, WORKERS + MP - 2)

    def send(c, carry):
        at = pl.multiple_of(c * chunk, 8)

        def to(worker, outer):
            target = worker * 4 + outer
            pltpu.make_async_remote_copy(
                src_ref=grads.at[pl.ds(pl.multiple_of(target * rows + at, 8), chunk)],
                dst_ref=held.at[me, pl.ds(at, chunk)],
                send_sem=sent,
                recv_sem=landed.at[c],
                device_id=(worker, outer, m),
                device_id_type=MESH,
            ).start()

        to(((high + 1) % 2) * 2 + core, o)
        for flip, step, other in send_order():
            to(((high + flip + core) % 2) * 2 + (core + other) % 2, (o + step) % 4)
        return carry

    lax.fori_loop(0, CHUNKS, send, 0)

    acc[...] = jnp.zeros_like(acc)
    own.wait()
    base.wait()

    def gather(c, carry):
        at = pl.multiple_of(c * chunk, 8)
        arrived = held.at[pl.ds(0, WORKERS - 1), pl.ds(at, chunk)]
        pltpu.make_async_copy(arrived, arrived, landed.at[c]).wait()

        def subtract(t, carry):
            here = pl.ds(pl.multiple_of(at + t * 8, 8), 8)
            v = start[here, :]
            for i in range(WORKERS):
                held[i, here, :] = held[i, here, :] - v
            return carry

        lax.fori_loop(0, chunk // 8, subtract, 0)
        for bi in range(WORKERS // BLOCK):
            for bj in range(bi, WORKERS // BLOCK):
                pairs = [(i, j) for i in range(bi * BLOCK, (bi + 1) * BLOCK) for j in range(bj * BLOCK, (bj + 1) * BLOCK) if i <= j]

                def products(t, sums, bi=bi, bj=bj, pairs=pairs):
                    here = pl.ds(pl.multiple_of(at + t * 8, 8), 8)
                    sums = list(sums)
                    for q in range(held.shape[2] // LANES):
                        there = slice(q * LANES, (q + 1) * LANES)
                        d = {i: held[i, here, there] for i in range(bi * BLOCK, (bi + 1) * BLOCK)}
                        for j in range(bj * BLOCK, (bj + 1) * BLOCK):
                            if j not in d:
                                d[j] = held[j, here, there]
                        for k, (i, j) in enumerate(pairs):
                            sums[k] = sums[k] + d[i] * d[j]
                    return tuple(sums)

                sums = lax.fori_loop(0, chunk // 8, products, tuple(acc[i * WORKERS + j] for i, j in pairs))
                for (i, j), total in zip(pairs, sums, strict=True):
                    acc[i * WORKERS + j] = total
        return carry

    lax.fori_loop(0, CHUNKS, gather, 0)

    for i in range(WORKERS):
        at = (i // 8) * LANES + ((8 - i % 8) % 8) * WORKERS
        for j in range(WORKERS):
            lines[at + j : at + j + 1, :] = jnp.sum(acc[min(i, j) * WORKERS + max(i, j)], axis=0, keepdims=True)
    across = lax.dot_general(
        jnp.full((8, LANES), 1.0, jnp.float32),
        lines[...] * 0.0625,
        (((1,), (1,)), ((), ())),
        precision=lax.Precision.HIGHEST,
        preferred_element_type=jnp.float32,
    )
    top = lax.broadcasted_iota(jnp.int32, (8, LANES), 0) == 0
    mine[...] = jnp.where(top, across[:, :LANES], across[:, LANES:]) * 16.0

    for k in range(1, WORKERS):
        pltpu.make_async_remote_copy(
            src_ref=mine, dst_ref=group.at[me], send_sem=scalar_sent.at[0], recv_sem=scalar_landed.at[0],
            device_id=((w + k // 4) % 4, (o + k % 4) % 4, m), device_id_type=MESH,
        ).start()
    group[me] = mine[...]
    arrived = group.at[pl.ds(0, WORKERS - 1)]
    pltpu.make_async_copy(arrived, arrived, scalar_landed.at[0]).wait()
    part = jnp.sum(group[...], axis=0)
    half[MP] = part
    for k in range(1, MP):
        pltpu.make_async_remote_copy(
            src_ref=half.at[MP], dst_ref=half.at[m], send_sem=scalar_sent.at[1], recv_sem=scalar_landed.at[1],
            device_id=(w, o, (m + k) % MP), device_id_type=MESH,
        ).start()
    half[m] = part
    pltpu.make_async_copy(held.at[pl.ds(0, WORKERS - 1)], held.at[pl.ds(0, WORKERS - 1)], sent).wait()
    pltpu.make_async_copy(arrived, arrived, scalar_sent.at[0]).wait()
    arrived = half.at[pl.ds(0, MP - 1)]
    pltpu.make_async_copy(arrived, arrived, scalar_landed.at[1]).wait()
    pltpu.make_async_copy(arrived, arrived, scalar_sent.at[1]).wait()
    total = jnp.sum(half[0:MP], axis=0)

    tables = [
        pltpu.roll(jnp.broadcast_to(total[h : h + 1, :], (8, LANES)), 0, 1, stride=WORKERS, stride_axis=0) for h in (0, 1)
    ]
    gram = jnp.concatenate(tables, axis=0)
    row = lax.broadcasted_iota(jnp.int32, (WORKERS, LANES), 0)
    column = lax.broadcasted_iota(jnp.int32, (WORKERS, LANES), 1)
    tau = radius[0] * math.sqrt(D * KVW)

    def share(squares):
        return jnp.minimum(1.0, tau * lax.rsqrt(squares + EPS)) * (1.0 / WORKERS)

    diagonal = jnp.where(row == column, gram, 0.0)
    squares = jnp.sum(diagonal, axis=1, keepdims=True)
    squares = jnp.where(squares < jnp.inf, squares, jnp.inf)
    squares_row = jnp.sum(diagonal, axis=0, keepdims=True)
    squares_row = jnp.where(squares_row < jnp.inf, squares_row, jnp.inf)
    first = share(squares)
    first_row = share(squares_row)
    used = jnp.logical_and(column < WORKERS, first_row > 0.0)
    along = jnp.sum(jnp.where(used, first_row * gram, 0.0), axis=1, keepdims=True)
    moved = jnp.sum(jnp.where(first > 0.0, first * along, 0.0), axis=0, keepdims=True)
    again = jnp.maximum(squares - 2.0 * along + moved, 0.0)
    again = jnp.where(squares < jnp.inf, again, jnp.inf)
    second = share(again)
    weight = first * (1.0 - jnp.sum(second, axis=0, keepdims=True)) + second
    bias[...] = jnp.broadcast_to(weight, (WORKERS, LANES))

    def combine(t, carry):
        here = pl.ds(pl.multiple_of(t * 8, 8), 8)
        for q in range(held.shape[2] // LANES):
            there = slice(q * LANES, (q + 1) * LANES)
            sums = [bias[i : i + 1, :] * held[i, here, there] for i in range(WORKERS)]
            while len(sums) > 1:
                sums = [a + b for a, b in zip(sums[::2], sums[1::2], strict=True)]
            out[here, there] = start[here, there] + sums[0]
        return carry

    lax.fori_loop(0, rows // 8, combine, 0)


def solution(mesh):
    def on_device(grads, center, radius):
        grads = grads.reshape(grads.shape[2], grads.shape[3])
        rows, columns = center.shape
        return pl.pallas_call(
            functools.partial(kernel, rows, rows // CHUNKS),
            out_shape=jax.ShapeDtypeStruct((rows, columns), jnp.float32),
            in_specs=[pl.BlockSpec(memory_space=pltpu.HBM), pl.BlockSpec(memory_space=pltpu.HBM), pl.BlockSpec(memory_space=pltpu.SMEM)],
            out_specs=pl.BlockSpec(memory_space=pltpu.VMEM),
            scratch_shapes=[
                pltpu.VMEM((WORKERS, rows, columns), jnp.float32),
                pltpu.VMEM((rows, columns), jnp.float32),
                pltpu.VMEM((WORKERS * WORKERS, 8, LANES), jnp.float32),
                pltpu.VMEM((WORKERS, LANES), jnp.float32),
                pltpu.VMEM((8, LANES), jnp.float32),
                pltpu.VMEM((WORKERS, 8, LANES), jnp.float32),
                pltpu.VMEM((MP + 1, 8, LANES), jnp.float32),
                pltpu.VMEM((WORKERS * WORKERS, LANES), jnp.float32),
                pltpu.SemaphoreType.DMA,
                pltpu.SemaphoreType.DMA((CHUNKS,)),
                pltpu.SemaphoreType.DMA((2,)),
                pltpu.SemaphoreType.DMA((2,)),
                pltpu.SemaphoreType.DMA((2,)),
            ],
            compiler_params=pltpu.CompilerParams(collective_id=0, has_side_effects=True, vmem_limit_bytes=60 * 2**20),
        )(grads, center, radius)

    return jax.shard_map(
        on_device,
        mesh=mesh,
        in_specs=(P("worker", "outer", None, "mp"), P(("worker", "outer"), "mp"), P()),
        out_specs=P(("worker", "outer"), "mp"),
        check_vma=False,
    )
```

time: 195 us -> 105 us (0.54)
  blocking collectives: 118 us -> 0 us
  Pallas kernels: 0 us -> 102 us
  waiting for transfers between devices: 50 us -> 0 us
  other arithmetic: 15.3 us -> 0 us
  local copies, waits for them, and re-layouts: 6.39 us -> 1.82 us
  starting transfers between devices: 4.5 us -> 0 us
    pallas_call x0 -> x1, Pallas kernels: none -> 102 us  [on_device(): pl.pallas_call(functools.partial(kernel, rows, rows // CHUNKS), out_shape...]
    psum x10 -> x0, blocking collectives: 64.4 us -> none  [over_axes(): return functools.reduce(lax.psum, axes, value)]
    all_to_all x1 -> x0, blocking collectives: 53.2 us -> none  [cut_exchange(): lax.all_to_all(section, axis, split_axis=0, concat_axis=0, tiled=True)]
    all_to_all x1 -> x0, waiting for transfers between devices: 50 us -> none  [cut_exchange(): lax.all_to_all(section, axis, split_axis=0, concat_axis=0, tiled=True)]
    reduce_sum x4 -> x0, other arithmetic: 14.3 us -> none  [the longest x2 7.9 us: on_device(): summed = jnp.sum(factor[:, None, None] * difference, axis=0)]
    split x1 -> x0, local copies, waits for them, and re-layouts: 6.36 us -> none  [cut_exchange(): jnp.split(blocks, piece_ends(blocks.shape[cut], pieces), axis=cut)]
    all_to_all x1 -> x0, starting transfers between devices: 4.5 us -> none  [cut_exchange(): lax.all_to_all(section, axis, split_axis=0, concat_axis=0, tiled=True)]
  transfers between devices with their start and end apart: 1 -> 0, of which waited for: 1 -> 0; matrix products, arithmetic and copies ran while one was open for 0% -> 0% of each run, Pallas kernels for 0% -> 0%
where the time goes in v1:
time: 105 us; the launch traced here: 104 us
  Pallas kernels  102 us (97%)
  local copies, waits for them, and re-layouts  1.82 us (2%)
    pallas_call x1, Pallas kernels, on_device(): pl.pallas_call(functools.partial(kernel, rows, rows // CHUNKS), out_shape...  102 us

profile of v1, /device:TPU:0, one launch (start us, length us, event | category | flops | bytes accessed | tf_op | source)
XLA Modules:
  0.0 104.1 jit_solution(1976807589621666227)
XLA Ops:
  0.7 101.6 %shard_map.37 = f32[224,512]{1,0:T(8,128)} custom-call(f32[3584,512]{1,0:T(8,128)} %bitcast.1, f32[224,512]{1,0:T(8,128)} %center.1, f32[1]{0:T(128)S(6)} %copy.5.radius), custom_call_target="tpu_custom_call" | custom-call | tf_op jit(solution)/shard_map/pallas_call | solution.py:193
  102.3 1.8 %copy.6 = f32[224,512]{1,0:T(8,128)} copy(f32[224,512]{1,0:T(8,128)} %shard_map.37) | data formatting | bytes 917504

commit v2 on v1

--- a/solution.py
+++ b/solution.py
@@ -12,25 +12,18 @@
 D = 3584
 KVW = 4096
 WORKERS = 16
-MP = 8
 EPS = 1e-06
-CHUNKS = 7
+CHUNKS = 14
 LANES = 128
 BLOCK = 4
 
 
-def send_order():
-    order = []
-    for core in (0, 1):
-        for flip in (0, 1):
-            for step in (1, 3, 2):
-                order.append((flip, step, core))
-            if core == 1:
-                order.append((flip, 0, core))
-    return order
-
-
-def kernel(rows, chunk, grads, center, radius, out, held, start, acc, bias, mine, group, half, lines, sent, landed, near, scalar_sent, scalar_landed):
+def far_chips():
+    chips = [(x, y, z) for x in range(4) for y in range(4) for z in range(4) if x or y or z]
+    return sorted(chips, key=lambda c: -sum(min(d, 4 - d) for d in c))
+
+
+def kernel(rows, chunk, grads, center, radius, out, held, start, acc, bias, mine, pair, both, every, lines, sent, landed, near, scalar_sent, scalar_landed, ready):
     w, o, m = lax.axis_index("worker"), lax.axis_index("outer"), lax.axis_index("mp")
     high, core = w // 2, w % 2
     me = w * 4 + o
@@ -40,33 +33,76 @@
     own.start()
     base.start()
 
+    def device(x, flip, other, y_low=0, z=0):
+        column = m // 4
+        return ((high + flip) % 2) * 2 + (core + other) % 2, (o + x) % 4, ((column + y_low) % 2) * 4 + (m % 4 + z) % 4
+
+    def greet(semaphore, *offsets):
+        pl.semaphore_signal(semaphore, inc=1, device_id=device(*offsets), device_id_type=MESH)
+
     barrier = pltpu.get_barrier_semaphore()
-    for k in range(1, WORKERS):
-        pl.semaphore_signal(barrier, inc=1, device_id=((w + k // 4) % 4, (o + k % 4) % 4, m), device_id_type=MESH)
-    for k in range(1, MP):
-        pl.semaphore_signal(barrier, inc=1, device_id=(w, o, (m + k) % MP), device_id_type=MESH)
-    pl.semaphore_wait(barrier, WORKERS + MP - 2)
-
-    def send(c, carry):
+    first_peers = [(x, 0, c) for x in (2, 1, 3) for c in (0, 1)] + [(0, 1, 0), (0, 1, 1), (0, 0, 1)]
+    first_peers += [(0, 0, 0, 0, 1), (0, 0, 0, 0, 3), (0, 0, 0, 1, 0)]
+    for offsets in first_peers:
+        greet(barrier, *offsets)
+    pl.semaphore_wait(barrier, len(first_peers))
+    greet(ready.at[0], 0, 1, 0)
+
+    def to(offsets, c):
+        worker, outer, part = device(*offsets)
+        target = worker * 4 + outer
         at = pl.multiple_of(c * chunk, 8)
-
-        def to(worker, outer):
-            target = worker * 4 + outer
-            pltpu.make_async_remote_copy(
-                src_ref=grads.at[pl.ds(pl.multiple_of(target * rows + at, 8), chunk)],
-                dst_ref=held.at[me, pl.ds(at, chunk)],
-                send_sem=sent,
-                recv_sem=landed.at[c],
-                device_id=(worker, outer, m),
-                device_id_type=MESH,
-            ).start()
-
-        to(((high + 1) % 2) * 2 + core, o)
-        for flip, step, other in send_order():
-            to(((high + flip + core) % 2) * 2 + (core + other) % 2, (o + step) % 4)
-        return carry
-
-    lax.fori_loop(0, CHUNKS, send, 0)
+        pltpu.make_async_remote_copy(
+            src_ref=grads.at[pl.ds(pl.multiple_of(target * rows + at, 8), chunk)],
+            dst_ref=held.at[me, pl.ds(at, chunk)],
+            send_sem=sent,
+            recv_sem=landed.at[c],
+            device_id=(worker, outer, part),
+            device_id_type=MESH,
+        ).start()
+
+    def send(flip, h):
+        for x in (1, 3, 2):
+            to((x, flip, h % 2), h // 2)
+
+        @pl.when(flip == 0)
+        def _():
+            to((0, 1, h % 2), h // 2)
+
+    last = 2 * CHUNKS - 1
+    send(0, 0)
+
+    @pl.when(core == 0)
+    def _():
+        send(0, 1)
+
+    pl.semaphore_wait(ready.at[0], 1)
+
+    @pl.when(core == 1)
+    def _():
+        send(1, 0)
+
+    def turn(s, carry):
+        before = s - 1
+        send((before + core) % 2, core * (s // 2) + (1 - core) * (before // 2 + 1 - before % 2))
+        return carry
+
+    lax.fori_loop(2, 2 * last + 1, turn, 0)
+    send(1, last)
+
+    def partner(c, carry):
+        to((0, 0, 1), c)
+        return carry
+
+    lax.fori_loop(0, CHUNKS, partner, 0)
+
+    greet(ready.at[1], 0, 0, 0, 1, 0)
+    pl.semaphore_wait(ready.at[1], 1)
+    greet(ready.at[2], 0, 0, 0, 0, 1)
+    greet(ready.at[2], 0, 0, 0, 0, 3)
+    pl.semaphore_wait(ready.at[2], 2)
+    greet(ready.at[3], 0, 0, 0, 0, 3)
+    pl.semaphore_wait(ready.at[3], 1)
 
     acc[...] = jnp.zeros_like(acc)
     own.wait()
@@ -121,30 +157,29 @@
         preferred_element_type=jnp.float32,
     )
     top = lax.broadcasted_iota(jnp.int32, (8, LANES), 0) == 0
-    mine[...] = jnp.where(top, across[:, :LANES], across[:, LANES:]) * 16.0
-
-    for k in range(1, WORKERS):
+    mine[...] = (jnp.where(top, across[:, :LANES], across[:, LANES:]) * 16.0)[0:2]
+
+    pltpu.make_async_remote_copy(
+        src_ref=mine, dst_ref=pair, send_sem=scalar_sent.at[0], recv_sem=scalar_landed.at[0],
+        device_id=device(0, 0, 1), device_id_type=MESH,
+    ).start()
+    pltpu.make_async_copy(pair, pair, scalar_landed.at[0]).wait()
+    both[...] = mine[...] + pair[...]
+    slot = (o * 4 + high * 2 + m // 4) * 4 + m % 4
+    y = high * 2 + m // 4
+    for dx, dy, dz in far_chips():
+        there = (y + dy) % 4
         pltpu.make_async_remote_copy(
-            src_ref=mine, dst_ref=group.at[me], send_sem=scalar_sent.at[0], recv_sem=scalar_landed.at[0],
-            device_id=((w + k // 4) % 4, (o + k % 4) % 4, m), device_id_type=MESH,
+            src_ref=both, dst_ref=every.at[slot], send_sem=scalar_sent.at[1], recv_sem=scalar_landed.at[1],
+            device_id=((there // 2) * 2 + core, (o + dx) % 4, (there % 2) * 4 + (m % 4 + dz) % 4), device_id_type=MESH,
         ).start()
-    group[me] = mine[...]
-    arrived = group.at[pl.ds(0, WORKERS - 1)]
-    pltpu.make_async_copy(arrived, arrived, scalar_landed.at[0]).wait()
-    part = jnp.sum(group[...], axis=0)
-    half[MP] = part
-    for k in range(1, MP):
-        pltpu.make_async_remote_copy(
-            src_ref=half.at[MP], dst_ref=half.at[m], send_sem=scalar_sent.at[1], recv_sem=scalar_landed.at[1],
-            device_id=(w, o, (m + k) % MP), device_id_type=MESH,
-        ).start()
-    half[m] = part
+    every[slot] = both[...]
     pltpu.make_async_copy(held.at[pl.ds(0, WORKERS - 1)], held.at[pl.ds(0, WORKERS - 1)], sent).wait()
-    pltpu.make_async_copy(arrived, arrived, scalar_sent.at[0]).wait()
-    arrived = half.at[pl.ds(0, MP - 1)]
+    pltpu.make_async_copy(pair, pair, scalar_sent.at[0]).wait()
+    arrived = every.at[pl.ds(0, 63)]
     pltpu.make_async_copy(arrived, arrived, scalar_landed.at[1]).wait()
     pltpu.make_async_copy(arrived, arrived, scalar_sent.at[1]).wait()
-    total = jnp.sum(half[0:MP], axis=0)
+    total = jnp.sum(every[...], axis=0)
 
     tables = [
         pltpu.roll(jnp.broadcast_to(total[h : h + 1, :], (8, LANES)), 0, 1, stride=WORKERS, stride_axis=0) for h in (0, 1)
@@ -192,7 +227,7 @@
         rows, columns = center.shape
         return pl.pallas_call(
             functools.partial(kernel, rows, rows // CHUNKS),
-            out_shape=jax.ShapeDtypeStruct((rows, columns), jnp.float32),
+            out_shape=pltpu.VMEM((rows, columns), jnp.float32),
             in_specs=[pl.BlockSpec(memory_space=pltpu.HBM), pl.BlockSpec(memory_space=pltpu.HBM), pl.BlockSpec(memory_space=pltpu.SMEM)],
             out_specs=pl.BlockSpec(memory_space=pltpu.VMEM),
             scratch_shapes=[
@@ -200,15 +235,17 @@
                 pltpu.VMEM((rows, columns), jnp.float32),
                 pltpu.VMEM((WORKERS * WORKERS, 8, LANES), jnp.float32),
                 pltpu.VMEM((WORKERS, LANES), jnp.float32),
-                pltpu.VMEM((8, LANES), jnp.float32),
-                pltpu.VMEM((WORKERS, 8, LANES), jnp.float32),
-                pltpu.VMEM((MP + 1, 8, LANES), jnp.float32),
+                pltpu.VMEM((2, LANES), jnp.float32),
+                pltpu.VMEM((2, LANES), jnp.float32),
+                pltpu.VMEM((2, LANES), jnp.float32),
+                pltpu.VMEM((64, 2, LANES), jnp.float32),
                 pltpu.VMEM((WORKERS * WORKERS, LANES), jnp.float32),
                 pltpu.SemaphoreType.DMA,
                 pltpu.SemaphoreType.DMA((CHUNKS,)),
                 pltpu.SemaphoreType.DMA((2,)),
                 pltpu.SemaphoreType.DMA((2,)),
                 pltpu.SemaphoreType.DMA((2,)),
+                pltpu.SemaphoreType.REGULAR((4,)),
             ],
             compiler_params=pltpu.CompilerParams(collective_id=0, has_side_effects=True, vmem_limit_bytes=60 * 2**20),
         )(grads, center, radius)

time: 105 us -> 101 us (0.962)
  Pallas kernels: 102 us -> 98 us
  local copies, waits for them, and re-layouts: 1.82 us -> 0.77 us
    pallas_call x1, Pallas kernels: 102 us -> 98 us  [on_device(): pl.pallas_call(functools.partial(kernel, rows, rows // CHUNKS), out_shape...]
where the time goes in v2:
time: 101 us; the launch traced here: 99.4 us
  Pallas kernels  98 us (97%)
    pallas_call x1, Pallas kernels, on_device(): pl.pallas_call(functools.partial(kernel, rows, rows // CHUNKS), out_shape...  98 us

profile of v2, /device:TPU:0, one launch (start us, length us, event | category | flops | bytes accessed | tf_op | source)
XLA Modules:
  0.0 99.4 jit_solution(7170629121756679441)
XLA Ops:
  0.7 98.0 %shard_map.37 = f32[224,512]{1,0:T(8,128)S(1)} custom-call(f32[3584,512]{1,0:T(8,128)} %bitcast.1, f32[224,512]{1,0:T(8,128)} %center.1, f32[1]{0:T(128)S(6)} %copy.6.radius), custom_call_target="tpu_custom_call" | custom-call | tf_op jit(solution)/shard_map/pallas_call | solution.py:228
  98.7 0.8 copy.5

commit v3 on v2

--- a/solution.py
+++ b/solution.py
@@ -41,12 +41,12 @@
         pl.semaphore_signal(semaphore, inc=1, device_id=device(*offsets), device_id_type=MESH)
 
     barrier = pltpu.get_barrier_semaphore()
-    first_peers = [(x, 0, c) for x in (2, 1, 3) for c in (0, 1)] + [(0, 1, 0), (0, 1, 1), (0, 0, 1)]
-    first_peers += [(0, 0, 0, 0, 1), (0, 0, 0, 0, 3), (0, 0, 0, 1, 0)]
-    for offsets in first_peers:
+    nearest = [(2, 0, 0), (0, 1, 0), (1, 0, 0), (3, 0, 0), (0, 0, 0, 0, 1), (0, 0, 0, 0, 3), (0, 0, 0, 1, 0), (0, 0, 1)]
+    for offsets in nearest:
         greet(barrier, *offsets)
-    pl.semaphore_wait(barrier, len(first_peers))
-    greet(ready.at[0], 0, 1, 0)
+    pl.semaphore_wait(barrier, len(nearest))
+    greet(ready.at[0], 0, 0, 1)
+    greet(ready.at[1], 0, 1, 0)
 
     def to(offsets, c):
         worker, outer, part = device(*offsets)
@@ -71,38 +71,44 @@
 
     last = 2 * CHUNKS - 1
     send(0, 0)
+    pl.semaphore_wait(ready.at[0], 1)
 
     @pl.when(core == 0)
     def _():
         send(0, 1)
 
-    pl.semaphore_wait(ready.at[0], 1)
+    pl.semaphore_wait(ready.at[1], 1)
+    greet(ready.at[2], 0, 0, 1)
 
     @pl.when(core == 1)
     def _():
         send(1, 0)
 
+    pl.semaphore_wait(ready.at[2], 1)
+
+    def partner(c, carry):
+        to((0, 0, 1), c)
+        return carry
+
+    lax.fori_loop(0, CHUNKS, partner, 0)
+
     def turn(s, carry):
         before = s - 1
         send((before + core) % 2, core * (s // 2) + (1 - core) * (before // 2 + 1 - before % 2))
         return carry
 
-    lax.fori_loop(2, 2 * last + 1, turn, 0)
+    lax.fori_loop(2, 2 * last - 1, turn, 0)
+    send(1, last - 1)
     send(1, last)
-
-    def partner(c, carry):
-        to((0, 0, 1), c)
-        return carry
-
-    lax.fori_loop(0, CHUNKS, partner, 0)
-
-    greet(ready.at[1], 0, 0, 0, 1, 0)
-    pl.semaphore_wait(ready.at[1], 1)
-    greet(ready.at[2], 0, 0, 0, 0, 1)
-    greet(ready.at[2], 0, 0, 0, 0, 3)
-    pl.semaphore_wait(ready.at[2], 2)
-    greet(ready.at[3], 0, 0, 0, 0, 3)
+    send(0, last)
+
+    greet(ready.at[3], 0, 0, 0, 1, 0)
     pl.semaphore_wait(ready.at[3], 1)
+    greet(ready.at[4], 0, 0, 0, 0, 1)
+    greet(ready.at[4], 0, 0, 0, 0, 3)
+    pl.semaphore_wait(ready.at[4], 2)
+    greet(ready.at[5], 0, 0, 0, 0, 3)
+    pl.semaphore_wait(ready.at[5], 1)
 
     acc[...] = jnp.zeros_like(acc)
     own.wait()
@@ -245,7 +251,7 @@
                 pltpu.SemaphoreType.DMA((2,)),
                 pltpu.SemaphoreType.DMA((2,)),
                 pltpu.SemaphoreType.DMA((2,)),
-                pltpu.SemaphoreType.REGULAR((4,)),
+                pltpu.SemaphoreType.REGULAR((6,)),
             ],
             compiler_params=pltpu.CompilerParams(collective_id=0, has_side_effects=True, vmem_limit_bytes=60 * 2**20),
         )(grads, center, radius)

time: 101 us -> 99.8 us (0.988)
  no operation moved by 1% of the time
where the time goes in v3:
time: 99.8 us; the launch traced here: 98.9 us
  Pallas kernels  97.4 us (98%)
    pallas_call x1, Pallas kernels, on_device(): pl.pallas_call(functools.partial(kernel, rows, rows // CHUNKS), out_shape...  97.4 us

profile of v3, /device:TPU:0, one launch (start us, length us, event | category | flops | bytes accessed | tf_op | source)
XLA Modules:
  0.0 98.9 jit_solution(6404110391815641488)
XLA Ops:
  0.7 97.4 %shard_map.37 = f32[224,512]{1,0:T(8,128)S(1)} custom-call(f32[3584,512]{1,0:T(8,128)} %bitcast.1, f32[224,512]{1,0:T(8,128)} %center.1, f32[1]{0:T(128)S(6)} %copy.6.radius), custom_call_target="tpu_custom_call" | custom-call | tf_op jit(solution)/shard_map/pallas_call | solution.py:234
  98.1 0.8 copy.5

commit v4 on v3

--- a/solution.py
+++ b/solution.py
@@ -18,12 +18,12 @@
 BLOCK = 4
 
 
-def far_chips():
-    chips = [(x, y, z) for x in range(4) for y in range(4) for z in range(4) if x or y or z]
-    return sorted(chips, key=lambda c: -sum(min(d, 4 - d) for d in c))
-
-
-def kernel(rows, chunk, grads, center, radius, out, held, start, acc, bias, mine, pair, both, every, lines, sent, landed, near, scalar_sent, scalar_landed, ready):
+def far_devices():
+    devices = [(x, y, z, c) for c in (0, 1) for x in range(4) for y in range(4) for z in range(4) if x or y or z or c]
+    return sorted(devices, key=lambda d: -sum(min(k, 4 - k) for k in d[:3]))
+
+
+def kernel(rows, chunk, grads, center, radius, out, held, start, acc, bias, mine, every, lines, sent, landed, near, scalar_sent, scalar_landed, ready):
     w, o, m = lax.axis_index("worker"), lax.axis_index("outer"), lax.axis_index("mp")
     high, core = w // 2, w % 2
     me = w * 4 + o
@@ -151,10 +151,14 @@
 
     lax.fori_loop(0, CHUNKS, gather, 0)
 
+    def line(i, j):
+        return (i // 8) * LANES + ((8 - i % 8) % 8) * WORKERS + j
+
     for i in range(WORKERS):
-        at = (i // 8) * LANES + ((8 - i % 8) % 8) * WORKERS
-        for j in range(WORKERS):
-            lines[at + j : at + j + 1, :] = jnp.sum(acc[min(i, j) * WORKERS + max(i, j)], axis=0, keepdims=True)
+        for j in range(i, WORKERS):
+            whole = jnp.sum(acc[i * WORKERS + j], axis=0, keepdims=True)
+            for at in sorted({line(i, j), line(j, i)}):
+                lines[at : at + 1, :] = whole
     across = lax.dot_general(
         jnp.full((8, LANES), 1.0, jnp.float32),
         lines[...] * 0.0625,
@@ -165,26 +169,19 @@
     top = lax.broadcasted_iota(jnp.int32, (8, LANES), 0) == 0
     mine[...] = (jnp.where(top, across[:, :LANES], across[:, LANES:]) * 16.0)[0:2]
 
-    pltpu.make_async_remote_copy(
-        src_ref=mine, dst_ref=pair, send_sem=scalar_sent.at[0], recv_sem=scalar_landed.at[0],
-        device_id=device(0, 0, 1), device_id_type=MESH,
-    ).start()
-    pltpu.make_async_copy(pair, pair, scalar_landed.at[0]).wait()
-    both[...] = mine[...] + pair[...]
-    slot = (o * 4 + high * 2 + m // 4) * 4 + m % 4
     y = high * 2 + m // 4
-    for dx, dy, dz in far_chips():
+    slot = ((o * 4 + y) * 4 + m % 4) * 2 + core
+    for dx, dy, dz, dc in far_devices():
         there = (y + dy) % 4
         pltpu.make_async_remote_copy(
-            src_ref=both, dst_ref=every.at[slot], send_sem=scalar_sent.at[1], recv_sem=scalar_landed.at[1],
-            device_id=((there // 2) * 2 + core, (o + dx) % 4, (there % 2) * 4 + (m % 4 + dz) % 4), device_id_type=MESH,
+            src_ref=mine, dst_ref=every.at[slot], send_sem=scalar_sent, recv_sem=scalar_landed,
+            device_id=((there // 2) * 2 + (core + dc) % 2, (o + dx) % 4, (there % 2) * 4 + (m % 4 + dz) % 4),
+            device_id_type=MESH,
         ).start()
-    every[slot] = both[...]
+    every[slot] = mine[...]
     pltpu.make_async_copy(held.at[pl.ds(0, WORKERS - 1)], held.at[pl.ds(0, WORKERS - 1)], sent).wait()
-    pltpu.make_async_copy(pair, pair, scalar_sent.at[0]).wait()
-    arrived = every.at[pl.ds(0, 63)]
-    pltpu.make_async_copy(arrived, arrived, scalar_landed.at[1]).wait()
-    pltpu.make_async_copy(arrived, arrived, scalar_sent.at[1]).wait()
+    arrived = every.at[pl.ds(0, 127)]
+    pltpu.make_async_copy(arrived, arrived, scalar_landed).wait()
     total = jnp.sum(every[...], axis=0)
 
     tables = [
@@ -214,17 +211,20 @@
     weight = first * (1.0 - jnp.sum(second, axis=0, keepdims=True)) + second
     bias[...] = jnp.broadcast_to(weight, (WORKERS, LANES))
 
+    weights = [jnp.broadcast_to(bias[i : i + 1, :], (8, LANES)) for i in range(WORKERS)]
+
     def combine(t, carry):
         here = pl.ds(pl.multiple_of(t * 8, 8), 8)
         for q in range(held.shape[2] // LANES):
             there = slice(q * LANES, (q + 1) * LANES)
-            sums = [bias[i : i + 1, :] * held[i, here, there] for i in range(WORKERS)]
+            sums = [weights[i] * held[i, here, there] for i in range(WORKERS)]
             while len(sums) > 1:
                 sums = [a + b for a, b in zip(sums[::2], sums[1::2], strict=True)]
             out[here, there] = start[here, there] + sums[0]
         return carry
 
-    lax.fori_loop(0, rows // 8, combine, 0)
+    lax.fori_loop(0, rows // 8, combine, 0, unroll=2)
+    pltpu.make_async_copy(arrived, arrived, scalar_sent).wait()
 
 
 def solution(mesh):
@@ -242,15 +242,13 @@
                 pltpu.VMEM((WORKERS * WORKERS, 8, LANES), jnp.float32),
                 pltpu.VMEM((WORKERS, LANES), jnp.float32),
                 pltpu.VMEM((2, LANES), jnp.float32),
-                pltpu.VMEM((2, LANES), jnp.float32),
-                pltpu.VMEM((2, LANES), jnp.float32),
-                pltpu.VMEM((64, 2, LANES), jnp.float32),
+                pltpu.VMEM((128, 2, LANES), jnp.float32),
                 pltpu.VMEM((WORKERS * WORKERS, LANES), jnp.float32),
                 pltpu.SemaphoreType.DMA,
                 pltpu.SemaphoreType.DMA((CHUNKS,)),
                 pltpu.SemaphoreType.DMA((2,)),
-                pltpu.SemaphoreType.DMA((2,)),
-                pltpu.SemaphoreType.DMA((2,)),
+                pltpu.SemaphoreType.DMA,
+                pltpu.SemaphoreType.DMA,
                 pltpu.SemaphoreType.REGULAR((6,)),
             ],
             compiler_params=pltpu.CompilerParams(collective_id=0, has_side_effects=True, vmem_limit_bytes=60 * 2**20),

time: 99.8 us -> 99.2 us (level)
  no operation moved by 1% of the time
where the time goes in v4:
time: 99.2 us; the launch traced here: 98.1 us
  Pallas kernels  96.7 us (97%)
    pallas_call x1, Pallas kernels, on_device(): pl.pallas_call(functools.partial(kernel, rows, rows // CHUNKS), out_shape...  96.7 us

profile of v4, /device:TPU:0, one launch (start us, length us, event | category | flops | bytes accessed | tf_op | source)
XLA Modules:
  0.0 98.1 jit_solution(10893185158470766503)
XLA Ops:
  0.7 96.7 %shard_map.37 = f32[224,512]{1,0:T(8,128)S(1)} custom-call(f32[3584,512]{1,0:T(8,128)} %bitcast.1, f32[224,512]{1,0:T(8,128)} %center.1, f32[1]{0:T(128)S(6)} %copy.6.radius), custom_call_target="tpu_custom_call" | custom-call | tf_op jit(solution)/shard_map/pallas_call | solution.py:234
  97.3 0.8 copy.5

commit v5 on v4

--- a/solution.py
+++ b/solution.py
@@ -20,7 +20,7 @@
 
 def far_devices():
     devices = [(x, y, z, c) for c in (0, 1) for x in range(4) for y in range(4) for z in range(4) if x or y or z or c]
-    return sorted(devices, key=lambda d: -sum(min(k, 4 - k) for k in d[:3]))
+    return sorted(devices, key=lambda d: (-sum(min(k, 4 - k) for k in d[:3]), -min(d[2], 4 - d[2])))
 
 
 def kernel(rows, chunk, grads, center, radius, out, held, start, acc, bias, mine, every, lines, sent, landed, near, scalar_sent, scalar_landed, ready):
@@ -182,7 +182,7 @@
     pltpu.make_async_copy(held.at[pl.ds(0, WORKERS - 1)], held.at[pl.ds(0, WORKERS - 1)], sent).wait()
     arrived = every.at[pl.ds(0, 127)]
     pltpu.make_async_copy(arrived, arrived, scalar_landed).wait()
-    total = jnp.sum(every[...], axis=0)
+    total = jnp.sum(jnp.sum(every[...].reshape(16, 8, 2, LANES), axis=0), axis=0)
 
     tables = [
         pltpu.roll(jnp.broadcast_to(total[h : h + 1, :], (8, LANES)), 0, 1, stride=WORKERS, stride_axis=0) for h in (0, 1)

time: 99.2 us -> 99.1 us (level)
  no operation moved by 1% of the time
where the time goes in v5:
time: 99.1 us; the launch traced here: 98.1 us
  Pallas kernels  96.6 us (97%)
    pallas_call x1, Pallas kernels, on_device(): pl.pallas_call(functools.partial(kernel, rows, rows // CHUNKS), out_shape...  96.6 us

profile of v5, /device:TPU:0, one launch (start us, length us, event | category | flops | bytes accessed | tf_op | source)
XLA Modules:
  0.0 98.1 jit_solution(13100106018172818261)
XLA Ops:
  0.7 96.6 %shard_map.37 = f32[224,512]{1,0:T(8,128)S(1)} custom-call(f32[3584,512]{1,0:T(8,128)} %bitcast.1, f32[224,512]{1,0:T(8,128)} %center.1, f32[1]{0:T(128)S(6)} %copy.6.radius), custom_call_target="tpu_custom_call" | custom-call | tf_op jit(solution)/shard_map/pallas_call | solution.py:234
  97.3 0.8 copy.5

commit v6 on v5

--- a/solution.py
+++ b/solution.py
@@ -30,8 +30,6 @@
 
     own = pltpu.make_async_copy(grads.at[pl.ds(pl.multiple_of(me * rows, 8), rows)], held.at[me], near.at[0])
     base = pltpu.make_async_copy(center, start, near.at[1])
-    own.start()
-    base.start()
 
     def device(x, flip, other, y_low=0, z=0):
         column = m // 4
@@ -44,6 +42,8 @@
     nearest = [(2, 0, 0), (0, 1, 0), (1, 0, 0), (3, 0, 0), (0, 0, 0, 0, 1), (0, 0, 0, 0, 3), (0, 0, 0, 1, 0), (0, 0, 1)]
     for offsets in nearest:
         greet(barrier, *offsets)
+    own.start()
+    base.start()
     pl.semaphore_wait(barrier, len(nearest))
     greet(ready.at[0], 0, 0, 1)
     greet(ready.at[1], 0, 1, 0)

time: 99.1 us -> 99.1 us (level)
  no operation moved by 1% of the time
where the time goes in v6:
time: 99.1 us; the launch traced here: 98 us
  Pallas kernels  96.6 us (97%)
    pallas_call x1, Pallas kernels, on_device(): pl.pallas_call(functools.partial(kernel, rows, rows // CHUNKS), out_shape...  96.6 us

profile of v6, /device:TPU:0, one launch (start us, length us, event | category | flops | bytes accessed | tf_op | source)
XLA Modules:
  0.0 98.0 jit_solution(1158866582327754945)
XLA Ops:
  0.7 96.6 %shard_map.37 = f32[224,512]{1,0:T(8,128)S(1)} custom-call(f32[3584,512]{1,0:T(8,128)} %bitcast.1, f32[224,512]{1,0:T(8,128)} %center.1, f32[1]{0:T(128)S(6)} %copy.6.radius), custom_call_target="tpu_custom_call" | custom-call | tf_op jit(solution)/shard_map/pallas_call | solution.py:234
  97.3 0.8 copy.5
